TPU v7x, 32 devices: a whole 2x2x4 slice. The times are simulated.
32 devices in a mesh: rep: 2 (over x), amp: 16 (over z, y, core).
Axes of the slice: x: 2, y: 2, z: 4, core: 2. Of those that a mesh axis runs over, the one named last changes fastest.
Arguments:
- amplitudes: float32 [2, 1048576], P(None, ('rep', 'amp')), parts along dimension 1, may hold values from -12 to 12
- coupling_index: int32 [4, 18], P('rep'), parts along dimension 0, may hold values from 0 to 15
- rotation_index: int32 [4, 19], P('rep'), parts along dimension 0, may hold values from 0 to 15
- chain_order: int32 [19], replicated, may hold values from 0 to 18, each once
- bond_sign: int32 [18], replicated, may hold values 0 or 1
Outputs:
- final_state: float32 [2, 1048576], P(None, ('rep', 'amp')), parts along dimension 1
- energies: float32 [4], P('rep'), parts along dimension 0
There are 2 independent parts, one for each index of `rep`. A program takes and returns all parts, laid end to end along the dimension named above; an argument that names none is the same for every part. Nothing has to cross between parts.
Inputs may be any that keep to these rules, and one draw needn't show every extreme that they name: chain_order holds each of 0 to 18 once.
All inputs are finite; a program needn't handle non-finite values.
Results may differ from a plain program's by a relative error of at most 0.0003.
Values sent between devices are 32-bit elements; how exact they have to be, the bound alone decides.
A program may use at most 128 MiB of HBM per device.

v0:
```python
import functools
import math

import jax
import jax.numpy as jnp
from jax import lax
from jax.experimental import pallas as pl
from jax.experimental.pallas import tpu as pltpu
from jax.sharding import PartitionSpec as P

LAYERS = 2
ANGLES = 16
LANES = 128
LANE_BITS = 7
F32 = jnp.float32
BF16 = jnp.bfloat16
MESH = pl.DeviceIdType.MESH


def angle(index):
    return (index + 1).astype(F32) * F32(math.pi / (2.0 * (ANGLES + 1)))


def mm(left, right):
    return jnp.dot(left, right, preferred_element_type=F32)


def split(values):
    high = values.astype(BF16)
    return high, (values - high.astype(F32)).astype(BF16)


def mm3(left, right):
    return mm(left[0], right[0]) + mm(left[1], right[0]) + mm(left[0], right[1])


def mm_exact_left(left, values):
    high = values.astype(BF16)
    rest = values - high.astype(F32)
    middle = rest.astype(BF16)
    low = (rest - middle.astype(F32)).astype(BF16)
    return mm(left, high) + mm(left, middle) + mm(left, low)


def mm_exact_right(values, right):
    high = values.astype(BF16)
    rest = values - high.astype(F32)
    middle = rest.astype(BF16)
    low = (rest - middle.astype(F32)).astype(BF16)
    return mm(high, right) + mm(middle, right) + mm(low, right)


def sin_cos(values):
    turns = jnp.floor(values * F32(1.0 / math.pi) + 0.5)
    rest = values - turns * F32(3.140625)
    rest = rest - turns * F32(9.67502593994140625e-4)
    rest = rest - turns * F32(1.509957990978376432e-7)
    sign = 1.0 - 2.0 * (turns - 2.0 * jnp.floor(turns * 0.5))
    square = rest * rest
    sine = F32(-1.0 / 39916800)
    for coefficient in (1.0 / 362880, -1.0 / 5040, 1.0 / 120, -1.0 / 6, 1.0):
        sine = sine * square + F32(coefficient)
    cosine = F32(-1.0 / 3628800)
    for coefficient in (1.0 / 40320, -1.0 / 720, 1.0 / 24, -0.5, 1.0):
        cosine = cosine * square + F32(coefficient)
    return sine * (rest * sign), cosine * sign


def gate_matrix(pairs):
    base = min(len(pairs), LANE_BITS)
    size = 2**base
    differ = lax.broadcasted_iota(jnp.int32, (size, size), 0) ^ lax.broadcasted_iota(
        jnp.int32, (size, size), 1
    )
    count = jnp.zeros((size, size), jnp.int32)
    value = jnp.ones((size, size), F32)
    for bit, (cosine, sine) in enumerate(pairs[:base]):
        flag = (differ >> bit) & 1
        count = count + flag
        value = value * jnp.where(flag == 1, sine, cosine)
    value = jnp.where(((count + 1) & 2) == 2, -value, value)
    odd = (count & 1) == 1
    real, imag = jnp.where(odd, 0.0, value), jnp.where(odd, value, 0.0)
    for cosine, sine in pairs[base:]:
        same_real, same_imag = cosine * real, cosine * imag
        flip_real, flip_imag = sine * imag, -sine * real

        def block(same, flip):
            return jnp.concatenate(
                [
                    jnp.concatenate([same, flip], axis=1),
                    jnp.concatenate([flip, same], axis=1),
                ],
                axis=0,
            )

        real, imag = block(same_real, flip_real), block(same_imag, flip_imag)
    return real, imag


def lane_operand(pairs):
    real, imag = gate_matrix(pairs)
    return split(
        jnp.concatenate(
            [jnp.concatenate([real, imag], axis=1), jnp.concatenate([-imag, real], axis=1)],
            axis=0,
        )
    )


def row_operand(pairs):
    return split(jnp.concatenate(gate_matrix(pairs), axis=0))


def apply_lanes(real, imag, operand):
    both = mm3(split(jnp.concatenate([real, imag], axis=1)), operand)
    return both[:, :LANES], both[:, LANES:]


def apply_rows(real, imag, operand):
    rows = real.shape[0]
    both = mm3(operand, split(jnp.concatenate([real, imag], axis=1)))
    return (
        both[:rows, :LANES] - both[rows:, LANES:],
        both[:rows, LANES:] + both[rows:, :LANES],
    )


def apply_top(real, imag, pairs, block_rows):
    rows = real.shape[0]
    if block_rows % 8:
        low = block_rows.bit_length() - 1
        pairs = [(F32(1.0), F32(0.0))] * low + pairs
        return apply_rows(real, imag, row_operand(pairs))
    for bit, (cosine, sine) in enumerate(pairs):
        width = block_rows << bit
        real_parts, imag_parts = [], []
        for start in range(0, rows, 2 * width):
            low, high = slice(start, start + width), slice(start + width, start + 2 * width)
            real_parts += [
                cosine * real[low] + sine * imag[high],
                cosine * real[high] + sine * imag[low],
            ]
            imag_parts += [
                cosine * imag[low] - sine * real[high],
                cosine * imag[high] - sine * real[low],
            ]
        real = jnp.concatenate(real_parts, axis=0)
        imag = jnp.concatenate(imag_parts, axis=0)
    return real, imag


def kernel(
    axis, count, chunks, qubits,
    state_hbm, couple_hbm, turn_hbm, order_hbm, sign_hbm,
    out_ref, energy_ref,
    state_ref, couple_ref, turn_ref, order_ref, sign_ref,
    table, send, recv, stat_send, stat_recv, plane_real, plane_imag,
    local_sems, send_sems, recv_sems, stat_send_sems, stat_recv_sems,
):
    me = lax.axis_index(axis)
    rows = state_ref.shape[0] // 2
    row_bits = rows.bit_length() - 1
    global_bits = count.bit_length() - 1
    local_bits = row_bits + LANE_BITS
    block_rows = rows // count
    low_bits = row_bits - global_bits
    chunk_bits = chunks.bit_length() - 1
    chunk_rows = block_rows // chunks
    inner_bits = low_bits - chunk_bits
    part_rows = rows // chunks
    order = sorted(range(1, count), key=lambda step: abs(count // 2 - step))
    peers = {step: lax.rem(me + step, count) for step in order}

    barrier = pltpu.get_barrier_semaphore()
    arrivals = [
        pltpu.make_async_copy(source, target, local_sems.at[number])
        for number, (source, target) in enumerate(
            [
                (couple_hbm, couple_ref),
                (turn_hbm, turn_ref),
                (order_hbm, order_ref),
                (sign_hbm, sign_ref),
                (state_hbm, state_ref),
            ]
        )
    ]
    for copy in arrivals:
        copy.start()

    for step in order:
        pl.semaphore_signal(barrier, inc=1, device_id={axis: peers[step]}, device_id_type=MESH)

    for entry in range(ANGLES):
        theta = (entry + 1) * math.pi / (2.0 * (ANGLES + 1))
        table[0, entry] = F32(math.cos(theta))
        table[1, entry] = F32(math.sin(theta))
    for copy in arrivals[:-1]:
        copy.wait()

    def turn(layer, qubit):
        index = turn_ref[layer, qubit]
        return table[0, index], table[1, index]

    height = -(-qubits // 8) * 8
    place = lax.broadcasted_iota(jnp.int32, (height, LANES), 0) * LANES + (
        lax.broadcasted_iota(jnp.int32, (height, LANES), 1)
    )

    def couplings(layers):
        matrices = [jnp.zeros((height, LANES), F32) for _ in layers]
        for bond in range(qubits - 1):
            start, end = order_ref[bond], order_ref[bond + 1]
            here = (place == start * LANES + end) | (place == end * LANES + start)
            for number, layer in enumerate(layers):
                value = (2 * sign_ref[bond] - 1).astype(F32)
                if layer < LAYERS:
                    value = angle(couple_ref[layer, bond]) * value
                matrices[number] = jnp.where(here, value, matrices[number])
        rest = jnp.zeros((LANES - height, LANES), F32)
        return [jnp.concatenate([matrix, rest], axis=0) for matrix in matrices]

    square_row = lax.broadcasted_iota(jnp.int32, (LANES, LANES), 0)
    square_lane = lax.broadcasted_iota(jnp.int32, (LANES, LANES), 1)
    lane_spin = (1 - 2 * ((square_lane >> jnp.minimum(square_row, 31)) & 1)).astype(F32)
    lane_only = jnp.where(square_row < LANE_BITS, lane_spin, 0.0)
    lane_ones = jnp.where(square_row < LANE_BITS, lane_spin, 1.0).astype(BF16)
    row_index = lax.broadcasted_iota(jnp.int32, (rows, LANES), 0)
    lane_index = lax.broadcasted_iota(jnp.int32, (rows, LANES), 1)

    def row_spin(swapped, chunked):
        held = row_index
        if chunked:
            inner = held & (chunk_rows - 1)
            block = (held >> inner_bits) & (count - 1)
            chunk = held >> (inner_bits + global_bits)
            held = inner + (chunk << inner_bits) + (block << low_bits)
        if swapped:
            low, high = held & (block_rows - 1), held >> low_bits
            index = low + (me << low_bits) + (high << row_bits)
        else:
            index = held + (me << row_bits)
        spin = (1 - 2 * ((index >> jnp.clip(lane_index - LANE_BITS, 0, 31)) & 1)).astype(F32)
        return jnp.where((lane_index >= LANE_BITS) & (lane_index < qubits), spin, 0.0)

    def field(spin, matrix, exact):
        if exact:
            half = mm(spin.astype(BF16), matrix.astype(BF16))
        else:
            half = mm_exact_left(spin.astype(BF16), matrix)
        half = jnp.where(lane_index < LANE_BITS, half, 0.5 * half * spin)
        lane_pairs = 0.5 * jnp.sum(
            mm_exact_right(matrix, lane_only.astype(BF16)) * lane_only, axis=0, keepdims=True
        )
        if exact:
            return mm(half.astype(BF16), lane_ones) + lane_pairs
        return mm_exact_right(half, lane_ones) + lane_pairs

    def copies(layer, chunk):
        return [
            pltpu.make_async_remote_copy(
                src_ref=send.at[layer, chunk, peers[step]],
                dst_ref=recv.at[layer, chunk, me],
                send_sem=send_sems.at[layer, chunk, step],
                recv_sem=recv_sems.at[layer, chunk, step],
                device_id={axis: peers[step]},
                device_id_type=MESH,
            )
            for step in order
        ]

    def stat_copies(which):
        return [
            pltpu.make_async_remote_copy(
                src_ref=stat_send.at[which],
                dst_ref=stat_recv.at[which, me],
                send_sem=stat_send_sems.at[which, step],
                recv_sem=stat_recv_sems.at[which, step],
                device_id={axis: peers[step]},
                device_id_type=MESH,
            )
            for step in order
        ]

    def pack(layer, chunk, real, imag, first_row, stride):
        for block in range(count):
            start = first_row + block * stride
            part = slice(start, start + chunk_rows)
            send[layer, chunk, block, :chunk_rows, :] = real[part]
            send[layer, chunk, block, chunk_rows:, :] = imag[part]

    def received(layer, chunk):
        if chunk_rows % 8 == 0:
            return (
                jnp.concatenate([recv[layer, chunk, b, :chunk_rows, :] for b in range(count)], axis=0),
                jnp.concatenate([recv[layer, chunk, b, chunk_rows:, :] for b in range(count)], axis=0),
            )
        for block in range(count):
            part = slice(block * chunk_rows, (block + 1) * chunk_rows)
            plane_real[part, :] = recv[layer, chunk, block, :chunk_rows, :]
            plane_imag[part, :] = recv[layer, chunk, block, chunk_rows:, :]
        return plane_real[...], plane_imag[...]

    def part_of(values, chunk):
        return values[chunk * part_rows : (chunk + 1) * part_rows]

    def turned(real, imag, pairs):
        return apply_top(real, imag, pairs, chunk_rows)

    sine, cosine = sin_cos(field(row_spin(False, False), couplings([0])[0], False))
    lanes = lane_operand([turn(0, qubit) for qubit in range(LANE_BITS)])
    held = row_operand([turn(0, LANE_BITS + bit) for bit in range(row_bits)])

    arrivals[-1].wait()
    real = state_ref[pl.ds(0, rows, 2), :]
    imag = state_ref[pl.ds(1, rows, 2), :]
    stat_send[0] = jnp.sum(real * real + imag * imag, axis=0, keepdims=True)
    real, imag = cosine * real + sine * imag, cosine * imag - sine * real
    real, imag = apply_lanes(real, imag, lanes)
    real, imag = apply_rows(real, imag, held)
    first = [copies(0, chunk) for chunk in range(chunks)]
    second = [copies(1, chunk) for chunk in range(chunks)]
    norms, weights = stat_copies(0), stat_copies(1)
    for chunk in range(chunks):
        pack(0, chunk, real, imag, chunk * chunk_rows, block_rows)
    pl.semaphore_wait(barrier, count - 1)
    for copy in first[0]:
        copy.start()
    for chunk in range(chunks):
        recv[0, chunk, me] = send[0, chunk, me]
    stat_recv[0, me] = stat_send[0]

    moved = row_spin(True, True)
    next_bonds, sign_bonds = couplings([1, LAYERS])
    sine, cosine = sin_cos(field(moved, next_bonds, False))
    for later in first[1:] + [norms]:
        for copy in later:
            copy.start()
    lanes = lane_operand([turn(1, qubit) for qubit in range(LANE_BITS)])
    held = row_operand(
        [turn(1, LANE_BITS + bit) for bit in range(inner_bits)]
        + [turn(1, local_bits + bit) for bit in range(global_bits)]
    )
    late = [turn(1, LANE_BITS + inner_bits + bit) for bit in range(chunk_bits)]
    tops = [
        [turn(0, local_bits + bit) for bit in range(global_bits)],
        [turn(1, local_bits - global_bits + bit) for bit in range(global_bits)],
    ]
    energy_moved = field(moved, sign_bonds, True)
    energy_plain = field(row_spin(False, True), sign_bonds, True)

    between = []
    for chunk in range(chunks):
        for copy in first[chunk]:
            copy.wait_recv()
        real, imag = received(0, chunk)
        real, imag = turned(real, imag, tops[0])
        between.append((real, imag))
        part_sine, part_cosine = part_of(sine, chunk), part_of(cosine, chunk)
        real, imag = (
            part_cosine * real + part_sine * imag,
            part_cosine * imag - part_sine * real,
        )
        real, imag = apply_lanes(real, imag, lanes)
        real, imag = apply_rows(real, imag, held)
        pack(1, chunk, real, imag, 0, chunk_rows)
        for copy in second[chunk]:
            copy.start()
        recv[1, chunk, me] = send[1, chunk, me]

    def folded(parts, energy_field):
        total = jnp.zeros((1, LANES), F32)
        for chunk, (real, imag) in enumerate(parts):
            weight = (real * real + imag * imag) * part_of(energy_field, chunk)
            total = total + jnp.sum(weight, axis=0, keepdims=True)
        return total + pltpu.roll(total, LANES // 2, 1)

    energy_first = folded(between, energy_moved)
    for copy in norms:
        copy.wait_recv()
    amps_total = F32(2.0**qubits)
    norm = jnp.sum(jnp.sum(stat_recv[0], axis=0), axis=1, keepdims=True)
    factor = 1.0 / jnp.sqrt(norm / amps_total + 1e-06)

    parts = []
    for chunk in range(chunks):
        for copy in second[chunk]:
            copy.wait_recv()
        real, imag = received(1, chunk)
        parts.append(turned(real, imag, tops[1]))
    for bit, (cosine, sine) in enumerate(late):
        fresh = list(parts)
        for low in range(chunks):
            high = low | 1 << bit
            if high == low:
                continue
            (low_real, low_imag), (high_real, high_imag) = parts[low], parts[high]
            fresh[low] = (cosine * low_real + sine * high_imag, cosine * low_imag - sine * high_real)
            fresh[high] = (cosine * high_real + sine * low_imag, cosine * high_imag - sine * low_real)
        parts = fresh

    lane = lax.broadcasted_iota(jnp.int32, (1, LANES), 1)
    stat_send[1] = jnp.where(lane < LANES // 2, energy_first, folded(parts, energy_plain))
    for copy in weights:
        copy.start()
    stat_recv[1, me] = stat_send[1]
    for chunk, (real, imag) in enumerate(parts):
        real, imag = real * factor, imag * factor
        for block in range(count):
            start = 2 * (block * block_rows + chunk * chunk_rows)
            part = slice(block * chunk_rows, (block + 1) * chunk_rows)
            out_ref[pl.ds(start, chunk_rows, 2), :] = real[part]
            out_ref[pl.ds(start + 1, chunk_rows, 2), :] = imag[part]
    for group in first + second + [norms]:
        for copy in group:
            copy.wait_send()
    for copy in weights:
        copy.wait_recv()
    sums = jnp.sum(stat_recv[1], axis=0) * (factor * factor / amps_total)
    low_sum = jnp.sum(jnp.where(lane < LANES // 2, sums, 0.0), axis=1, keepdims=True)
    high_sum = jnp.sum(jnp.where(lane < LANES // 2, 0.0, sums), axis=1, keepdims=True)
    which = lax.broadcasted_iota(jnp.int32, (1, LAYERS), 1)
    energy_ref[...] = jnp.where(which == 0, low_sum, high_sum)
    for copy in weights:
        copy.wait_send()


def solution(mesh):
    axis = "amp"
    count = mesh.shape[axis]

    def local(amplitudes, coupling_index, rotation_index, chain_order, bond_sign):
        rows = amplitudes.shape[1] // LANES
        qubits = chain_order.shape[0]
        block_rows = rows // count
        chunks = 2 if block_rows % 16 == 0 else 1
        chunk_rows = block_rows // chunks
        view = amplitudes.reshape(2, rows, LANES).transpose(1, 0, 2).reshape(2 * rows, LANES)
        vmem = pl.BlockSpec(memory_space=pltpu.VMEM)
        anywhere = pl.BlockSpec(memory_space=pl.ANY)
        state, energies = pl.pallas_call(
            functools.partial(kernel, axis, count, chunks, qubits),
            out_shape=(
                pltpu.VMEM((2 * rows, LANES), F32),
                pltpu.VMEM((1, LAYERS), F32),
            ),
            in_specs=[anywhere] * 5,
            out_specs=(vmem, vmem),
            scratch_shapes=[
                pltpu.VMEM((2 * rows, LANES), F32),
                pltpu.SMEM(coupling_index.shape, jnp.int32),
                pltpu.SMEM(rotation_index.shape, jnp.int32),
                pltpu.SMEM(chain_order.shape, jnp.int32),
                pltpu.SMEM(bond_sign.shape, jnp.int32),
                pltpu.SMEM((2, ANGLES), F32),
                pltpu.VMEM((LAYERS, chunks, count, 2 * chunk_rows, LANES), F32),
                pltpu.VMEM((LAYERS, chunks, count, 2 * chunk_rows, LANES), F32),
                pltpu.VMEM((2, 1, LANES), F32),
                pltpu.VMEM((2, count, 1, LANES), F32),
                pltpu.VMEM((rows, LANES), F32),
                pltpu.VMEM((rows, LANES), F32),
                pltpu.SemaphoreType.DMA((5,)),
                pltpu.SemaphoreType.DMA((LAYERS, chunks, count)),
                pltpu.SemaphoreType.DMA((LAYERS, chunks, count)),
                pltpu.SemaphoreType.DMA((2, count)),
                pltpu.SemaphoreType.DMA((2, count)),
            ],
            compiler_params=pltpu.CompilerParams(collective_id=0, has_side_effects=True),
        )(view, coupling_index, rotation_index, chain_order, bond_sign)
        state = state.reshape(rows, 2, LANES).transpose(1, 0, 2).reshape(2, rows * LANES)
        return state, energies.reshape(LAYERS)

    in_specs = (P(None, ("rep", "amp")), P("rep", None), P("rep", None), P(), P())
    out_specs = (P(None, ("rep", "amp")), P("rep"))
    return jax.shard_map(local, mesh=mesh, in_specs=in_specs, out_specs=out_specs, check_vma=False)
```

profile of v0, /device:TPU:0, one launch (start us, length us, event | category | flops | bytes accessed | tf_op | source)
XLA Modules:
  0.0 27.8 jit_solution(14639839024373047462)
XLA Ops:
  0.6 26.0 %shard_map.68 = (f32[512,128]{1,0:T(8,128)S(1)}, f32[1,2]{1,0:T(1,128)S(1)}) custom-call(f32[512,128]{1,0:T(8,128)} %bitcast.13, s32[2,18]{1,0:T(2,128)} %couple_hbm.1, s32[2,19]{1,0:T(2,128)} %turn_hbm.1, s32[19]{0:T(128)} %order_hbm.1, s32[18]{0:T(128)} %sign_hbm.1), custom_call_target="tpu_custom_call" | custom-call | tf_op jit(solution)/shard_map/pallas_call | solution.py:441
  26.6 0.7 %copy.11 = f32[2,32768]{1,0:T(2,128)} copy(f32[2,32768]{1,0:T(2,128)S(1)} %bitcast.11) | data formatting | bytes 524288
  27.3 0.5 %copy.12 = f32[2]{0:T(128)} copy(f32[2]{0:T(128)S(1)} %bitcast.12) | data formatting | bytes 16
where the time goes:
time: 28 us; the launch traced here: 27.8 us
  Pallas kernels  26 us (93%)
  local copies, waits for them, and re-layouts  1.22 us (4%)
  between operations  0.64 us (2%)
    pallas_call x1, Pallas kernels, local(): pl.pallas_call(functools.partial(kernel, axis, count, chunks, qubits), ou...  26 us
    unnamed x2, local copies, waits for them, and re-layouts  1.22 us

commit v1 on v0

--- a/solution.py
+++ b/solution.py
@@ -261,8 +261,8 @@
             pltpu.make_async_remote_copy(
                 src_ref=send.at[layer, chunk, peers[step]],
                 dst_ref=recv.at[layer, chunk, me],
-                send_sem=send_sems.at[layer, chunk, step],
-                recv_sem=recv_sems.at[layer, chunk, step],
+                send_sem=send_sems.at[layer, chunk],
+                recv_sem=recv_sems.at[layer, chunk],
                 device_id={axis: peers[step]},
                 device_id_type=MESH,
             )
@@ -274,13 +274,35 @@
             pltpu.make_async_remote_copy(
                 src_ref=stat_send.at[which],
                 dst_ref=stat_recv.at[which, me],
-                send_sem=stat_send_sems.at[which, step],
-                recv_sem=stat_recv_sems.at[which, step],
+                send_sem=stat_send_sems.at[which],
+                recv_sem=stat_recv_sems.at[which],
                 device_id={axis: peers[step]},
                 device_id_type=MESH,
             )
             for step in order
         ]
+
+    others = pl.ds(0, count - 1)
+
+    def blocks(layer, chunk):
+        return pltpu.make_async_remote_copy(
+            src_ref=send.at[layer, chunk, others],
+            dst_ref=recv.at[layer, chunk, others],
+            send_sem=send_sems.at[layer, chunk],
+            recv_sem=recv_sems.at[layer, chunk],
+            device_id={axis: peers[order[0]]},
+            device_id_type=MESH,
+        )
+
+    def stats(which):
+        return pltpu.make_async_remote_copy(
+            src_ref=stat_recv.at[which, others],
+            dst_ref=stat_recv.at[which, others],
+            send_sem=stat_send_sems.at[which],
+            recv_sem=stat_recv_sems.at[which],
+            device_id={axis: peers[order[0]]},
+            device_id_type=MESH,
+        )
 
     def pack(layer, chunk, real, imag, first_row, stride):
         for block in range(count):
@@ -351,8 +373,7 @@
 
     between = []
     for chunk in range(chunks):
-        for copy in first[chunk]:
-            copy.wait_recv()
+        blocks(0, chunk).wait_recv()
         real, imag = received(0, chunk)
         real, imag = turned(real, imag, tops[0])
         between.append((real, imag))
@@ -376,16 +397,14 @@
         return total + pltpu.roll(total, LANES // 2, 1)
 
     energy_first = folded(between, energy_moved)
-    for copy in norms:
-        copy.wait_recv()
+    stats(0).wait_recv()
     amps_total = F32(2.0**qubits)
     norm = jnp.sum(jnp.sum(stat_recv[0], axis=0), axis=1, keepdims=True)
     factor = 1.0 / jnp.sqrt(norm / amps_total + 1e-06)
 
     parts = []
     for chunk in range(chunks):
-        for copy in second[chunk]:
-            copy.wait_recv()
+        blocks(1, chunk).wait_recv()
         real, imag = received(1, chunk)
         parts.append(turned(real, imag, tops[1]))
     for bit, (cosine, sine) in enumerate(late):
@@ -411,18 +430,17 @@
             part = slice(block * chunk_rows, (block + 1) * chunk_rows)
             out_ref[pl.ds(start, chunk_rows, 2), :] = real[part]
             out_ref[pl.ds(start + 1, chunk_rows, 2), :] = imag[part]
-    for group in first + second + [norms]:
-        for copy in group:
-            copy.wait_send()
-    for copy in weights:
-        copy.wait_recv()
+    for layer in range(LAYERS):
+        for chunk in range(chunks):
+            blocks(layer, chunk).wait_send()
+    stats(0).wait_send()
+    stats(1).wait_recv()
     sums = jnp.sum(stat_recv[1], axis=0) * (factor * factor / amps_total)
     low_sum = jnp.sum(jnp.where(lane < LANES // 2, sums, 0.0), axis=1, keepdims=True)
     high_sum = jnp.sum(jnp.where(lane < LANES // 2, 0.0, sums), axis=1, keepdims=True)
     which = lax.broadcasted_iota(jnp.int32, (1, LAYERS), 1)
     energy_ref[...] = jnp.where(which == 0, low_sum, high_sum)
-    for copy in weights:
-        copy.wait_send()
+    stats(1).wait_send()
 
 
 def solution(mesh):
@@ -460,10 +478,10 @@
                 pltpu.VMEM((rows, LANES), F32),
                 pltpu.VMEM((rows, LANES), F32),
                 pltpu.SemaphoreType.DMA((5,)),
-                pltpu.SemaphoreType.DMA((LAYERS, chunks, count)),
-                pltpu.SemaphoreType.DMA((LAYERS, chunks, count)),
-                pltpu.SemaphoreType.DMA((2, count)),
-                pltpu.SemaphoreType.DMA((2, count)),
+                pltpu.SemaphoreType.DMA((LAYERS, chunks)),
+                pltpu.SemaphoreType.DMA((LAYERS, chunks)),
+                pltpu.SemaphoreType.DMA((2,)),
+                pltpu.SemaphoreType.DMA((2,)),
             ],
             compiler_params=pltpu.CompilerParams(collective_id=0, has_side_effects=True),
         )(view, coupling_index, rotation_index, chain_order, bond_sign)

time: 28 us -> 26.3 us (0.939)
  Pallas kernels: 26 us -> 24.3 us
    pallas_call x1, Pallas kernels: 26 us -> 24.3 us  [local(): pl.pallas_call(functools.partial(kernel, axis, count, chunks, qubits), ou...]
where the time goes in v1:
time: 26.3 us; the launch traced here: 26.1 us
  Pallas kernels  24.3 us (92%)
  local copies, waits for them, and re-layouts  1.22 us (5%)
  between operations  0.64 us (2%)
    pallas_call x1, Pallas kernels, local(): pl.pallas_call(functools.partial(kernel, axis, count, chunks, qubits), ou...  24.3 us
    unnamed x2, local copies, waits for them, and re-layouts  1.22 us

profile of v1, /device:TPU:0, one launch (start us, length us, event | category | flops | bytes accessed | tf_op | source)
XLA Modules:
  0.0 26.1 jit_solution(11627407152517798239)
XLA Ops:
  0.6 24.3 %shard_map.68 = (f32[512,128]{1,0:T(8,128)S(1)}, f32[1,2]{1,0:T(1,128)S(1)}) custom-call(f32[512,128]{1,0:T(8,128)} %bitcast.13, s32[2,18]{1,0:T(2,128)} %couple_hbm.1, s32[2,19]{1,0:T(2,128)} %turn_hbm.1, s32[19]{0:T(128)} %order_hbm.1, s32[18]{0:T(128)} %sign_hbm.1), custom_call_target="tpu_custom_call" | custom-call | tf_op jit(solution)/shard_map/pallas_call | solution.py:459
  24.9 0.7 %copy.11 = f32[2,32768]{1,0:T(2,128)} copy(f32[2,32768]{1,0:T(2,128)S(1)} %bitcast.11) | data formatting | bytes 524288
  25.6 0.5 %copy.12 = f32[2]{0:T(128)} copy(f32[2]{0:T(128)S(1)} %bitcast.12) | data formatting | bytes 16

commit v2 on v1

--- a/solution.py
+++ b/solution.py
@@ -15,6 +15,11 @@
 F32 = jnp.float32
 BF16 = jnp.bfloat16
 MESH = pl.DeviceIdType.MESH
+DOWN = (3, 2, 1, 0)
+PLANS = (
+    (((2, 3, 1, 0), (2, 0, 3, 1)), ((1, 0, 2, 3), DOWN)),
+    (((2, 3, 1, 0), DOWN), ((2, 3, 0, 1), DOWN)),
+)
 
 
 def angle(index):
@@ -169,8 +174,23 @@
     chunk_rows = block_rows // chunks
     inner_bits = low_bits - chunk_bits
     part_rows = rows // chunks
-    order = sorted(range(1, count), key=lambda step: abs(count // 2 - step))
-    peers = {step: lax.rem(me + step, count) for step in order}
+    def ranked(groups, inner):
+        size = count // 4
+        steps = [
+            group * size + high * (size // 4) + low
+            for group in groups
+            for high in inner
+            for low in range(size // 4)
+        ]
+        return [step for step in steps if step]
+
+    order = ranked((2, 3, 1, 0), (3, 2, 1, 0))
+    plans = [[ranked(*plan) for plan in layer] for layer in PLANS]
+    flips = [(1 - 2 * lax.rem(me // 2**bit, 2)) * 2**bit for bit in range(global_bits)]
+    peers = {
+        step: me + sum(flips[bit] for bit in range(global_bits) if step >> bit & 1)
+        for step in order
+    }
 
     barrier = pltpu.get_barrier_semaphore()
     arrivals = [
@@ -266,7 +286,7 @@
                 device_id={axis: peers[step]},
                 device_id_type=MESH,
             )
-            for step in order
+            for step in plans[layer][chunk]
         ]
 
     def stat_copies(which):
@@ -355,9 +375,12 @@
     moved = row_spin(True, True)
     next_bonds, sign_bonds = couplings([1, LAYERS])
     sine, cosine = sin_cos(field(moved, next_bonds, False))
-    for later in first[1:] + [norms]:
-        for copy in later:
+    for chunk in range(1, chunks):
+        blocks(0, chunk - 1).wait_send()
+        for copy in first[chunk]:
             copy.start()
+    for copy in norms:
+        copy.start()
     lanes = lane_operand([turn(1, qubit) for qubit in range(LANE_BITS)])
     held = row_operand(
         [turn(1, LANE_BITS + bit) for bit in range(inner_bits)]
@@ -430,9 +453,9 @@
             part = slice(block * chunk_rows, (block + 1) * chunk_rows)
             out_ref[pl.ds(start, chunk_rows, 2), :] = real[part]
             out_ref[pl.ds(start + 1, chunk_rows, 2), :] = imag[part]
-    for layer in range(LAYERS):
-        for chunk in range(chunks):
-            blocks(layer, chunk).wait_send()
+    blocks(0, chunks - 1).wait_send()
+    for chunk in range(chunks):
+        blocks(1, chunk).wait_send()
     stats(0).wait_send()
     stats(1).wait_recv()
     sums = jnp.sum(stat_recv[1], axis=0) * (factor * factor / amps_total)
@@ -441,6 +464,17 @@
     which = lax.broadcasted_iota(jnp.int32, (1, LAYERS), 1)
     energy_ref[...] = jnp.where(which == 0, low_sum, high_sum)
     stats(1).wait_send()
+
+
+def place(state_ref, energy_ref, state_out, energy_out, sems):
+    moves = [
+        pltpu.make_async_copy(state_ref, state_out, sems.at[0]),
+        pltpu.make_async_copy(energy_ref, energy_out, sems.at[1]),
+    ]
+    for move in moves:
+        move.start()
+    for move in moves:
+        move.wait()
 
 
 def solution(mesh):
@@ -485,6 +519,16 @@
             ],
             compiler_params=pltpu.CompilerParams(collective_id=0, has_side_effects=True),
         )(view, coupling_index, rotation_index, chain_order, bond_sign)
+        state, energies = pl.pallas_call(
+            place,
+            out_shape=(
+                jax.ShapeDtypeStruct((2 * rows, LANES), F32),
+                jax.ShapeDtypeStruct((1, LAYERS), F32),
+            ),
+            in_specs=[anywhere] * 2,
+            out_specs=(anywhere, anywhere),
+            scratch_shapes=[pltpu.SemaphoreType.DMA((2,))],
+        )(*(pltpu.with_memory_space_constraint(x, pltpu.VMEM) for x in (state, energies)))
         state = state.reshape(rows, 2, LANES).transpose(1, 0, 2).reshape(2, rows * LANES)
         return state, energies.reshape(LAYERS)
 

time: 26.3 us -> 24.9 us (0.947)
  local copies, waits for them, and re-layouts: 1.22 us -> 0 us
    unnamed x2 -> x0, local copies, waits for them, and re-layouts: 1.22 us -> none
    pallas_call x1, Pallas kernels: 24.3 us -> 23.4 us  [local(): pl.pallas_call(functools.partial(kernel, axis, count, chunks, qubits), ou...]
    pallas_call x0 -> x1, Pallas kernels: none -> 0.72 us  [local(): pl.pallas_call(place, out_shape=(jax.ShapeDtypeStruct((2 * rows, LANES),...]
where the time goes in v2:
time: 24.9 us; the launch traced here: 24.8 us
  Pallas kernels  24.1 us (97%)
  between operations  0.64 us (3%)
    pallas_call x1, Pallas kernels, local(): pl.pallas_call(functools.partial(kernel, axis, count, chunks, qubits), ou...  23.4 us
    pallas_call x1, Pallas kernels, local(): pl.pallas_call(place, out_shape=(jax.ShapeDtypeStruct((2 * rows, LANES),...  0.72 us

profile of v2, /device:TPU:0, one launch (start us, length us, event | category | flops | bytes accessed | tf_op | source)
XLA Modules:
  0.0 24.8 jit_solution(16592856279695337933)
XLA Ops:
  0.6 23.4 %shard_map.68 = (f32[512,128]{1,0:T(8,128)S(1)}, f32[1,2]{1,0:T(1,128)S(1)}) custom-call(f32[512,128]{1,0:T(8,128)} %bitcast.11, s32[2,18]{1,0:T(2,128)} %couple_hbm.1, s32[2,19]{1,0:T(2,128)} %turn_hbm.1, s32[19]{0:T(128)} %order_hbm.1, s32[18]{0:T(128)} %sign_hbm.1), custom_call_target="tpu_custom_call" | custom-call | tf_op jit(solution)/shard_map/pallas_call | solution.py:493
  24.1 0.7 %shard_map.69 = (f32[512,128]{1,0:T(8,128)}, f32[1,2]{1,0:T(1,128)}) custom-call(f32[512,128]{1,0:T(8,128)S(1)} %get-tuple-element.6.state_ref, f32[1,2]{1,0:T(1,128)S(1)} %get-tuple-element.7.energy_ref), custom_call_target="tpu_custom_call" | custom-call | tf_op jit(solution)/shard_map/pallas_call | solution.py:522

commit v3 on v2

v3 whole, which is shorter than its diff:
```python
import functools
import math

import jax
import jax.numpy as jnp
from jax import lax
from jax.experimental import pallas as pl
from jax.experimental.pallas import tpu as pltpu
from jax.sharding import PartitionSpec as P

LAYERS = 2
ANGLES = 16
LANES = 128
LANE_BITS = 7
TILE = 8
F32 = jnp.float32
BF16 = jnp.bfloat16
MESH = pl.DeviceIdType.MESH
DOWN = (3, 2, 1, 0)
PLANS = (
    (((2, 3, 1, 0), (2, 0, 3, 1)), ((1, 0, 2, 3), DOWN)),
    (((2, 3, 1, 0), DOWN), ((2, 3, 0, 1), DOWN)),
)


def angle(index):
    return (index + 1).astype(F32) * F32(math.pi / (2.0 * (ANGLES + 1)))


def mm(left, right):
    return jnp.dot(left, right, preferred_element_type=F32)


def split(values):
    high = values.astype(BF16)
    return high, (values - high.astype(F32)).astype(BF16)


def mm3(left, right):
    return mm(left[0], right[0]) + mm(left[1], right[0]) + mm(left[0], right[1])


def mm_exact_left(left, values):
    high = values.astype(BF16)
    rest = values - high.astype(F32)
    middle = rest.astype(BF16)
    low = (rest - middle.astype(F32)).astype(BF16)
    return mm(left, high) + mm(left, middle) + mm(left, low)


def mm_exact_right(values, right):
    high = values.astype(BF16)
    rest = values - high.astype(F32)
    middle = rest.astype(BF16)
    low = (rest - middle.astype(F32)).astype(BF16)
    return mm(high, right) + mm(middle, right) + mm(low, right)


def sin_cos(values):
    turns = jnp.floor(values * F32(1.0 / math.pi) + 0.5)
    rest = values - turns * F32(3.140625)
    rest = rest - turns * F32(9.67502593994140625e-4)
    rest = rest - turns * F32(1.509957990978376432e-7)
    sign = 1.0 - 2.0 * (turns - 2.0 * jnp.floor(turns * 0.5))
    square = rest * rest
    sine = F32(-1.0 / 39916800)
    for coefficient in (1.0 / 362880, -1.0 / 5040, 1.0 / 120, -1.0 / 6, 1.0):
        sine = sine * square + F32(coefficient)
    cosine = F32(-1.0 / 3628800)
    for coefficient in (1.0 / 40320, -1.0 / 720, 1.0 / 24, -0.5, 1.0):
        cosine = cosine * square + F32(coefficient)
    return sine * (rest * sign), cosine * sign


def rotation(pairs, transposed=False):
    base = min(len(pairs), LANE_BITS)
    shape = (TILE, 2**base)
    row = lax.broadcasted_iota(jnp.int32, shape, 0)
    column = lax.broadcasted_iota(jnp.int32, shape, 1)

    def factors(bit):
        pair = pairs[bit]
        cosine, sine = (F32(1.0), F32(0.0)) if pair is None else pair
        if transposed:
            sine = -sine
        here = ((column >> bit) & 1) == 1
        return jnp.where(here, -sine, cosine), jnp.where(here, cosine, sine)

    value = None
    for bit in range(3):
        clear, put = factors(bit)
        factor = jnp.where(((row >> bit) & 1) == 1, put, clear)
        value = factor if value is None else value * factor
    found = [value]
    for bit in range(3, base):
        clear, put = factors(bit)
        found = [value * clear for value in found] + [value * put for value in found]
    value = jnp.concatenate(found, axis=0)
    for cosine, sine in pairs[base:]:
        value = jnp.concatenate(
            [
                jnp.concatenate([cosine * value, -sine * value], axis=1),
                jnp.concatenate([sine * value, cosine * value], axis=1),
            ],
            axis=0,
        )
    return value


def right_operand(matrix):
    high, low = split(matrix)
    return jnp.concatenate(
        [
            jnp.concatenate([high, low], axis=1),
            jnp.concatenate([high, jnp.zeros_like(high)], axis=1),
        ],
        axis=0,
    )


def paired(left, right):
    both = mm(left, right)
    return both[:, :LANES] + both[:, LANES:]


def apply_lanes(values, operand):
    return paired(jnp.concatenate(split(values), axis=1), operand)


def turn_blocks(values, pairs):
    height = values.shape[0]
    for bit, (cosine, sine) in enumerate(pairs):
        width = TILE << bit
        parts = []
        for start in range(0, height, 2 * width):
            low = values[start : start + width]
            high = values[start + width : start + 2 * width]
            parts += [cosine * low - sine * high, cosine * high + sine * low]
        values = jnp.concatenate(parts, axis=0)
    return values


def flipped(values):
    groups = values.reshape(values.shape[0] // TILE, TILE, LANES)
    return pltpu.roll(groups, TILE // 2, 1).reshape(values.shape)


def kernel(
    axis, count, chunks, depth, qubits,
    state_hbm, couple_hbm, turn_hbm, order_hbm, sign_hbm,
    out_ref, energy_ref,
    state_ref, couple_ref, turn_ref, order_ref, sign_ref,
    table, send, recv, norm_send, norm_recv, energy_send, energy_recv,
    local_sems, send_sem, recv_sems, stat_send_sems, stat_recv_sems, near_sem, far_sem,
):
    me = lax.axis_index(axis)
    rows = state_ref.shape[0] // 2
    row_bits = rows.bit_length() - 1
    global_bits = count.bit_length() - 1
    local_bits = row_bits + LANE_BITS
    block_rows = rows // count
    low_bits = row_bits - global_bits
    chunk_bits = chunks.bit_length() - 1
    chunk_rows = block_rows // chunks
    inner_bits = low_bits - chunk_bits
    tiles = rows // chunk_rows
    units = chunks // depth
    def ranked(groups, inner):
        size = count // 4
        steps = [
            group * size + high * (size // 4) + low
            for group in groups
            for high in inner
            for low in range(size // 4)
        ]
        return [step for step in steps if step]

    order = ranked((2, 3, 1, 0), (3, 2, 1, 0))
    plans = [[ranked(*plan) for plan in layer] for layer in PLANS]
    flips = [(1 - 2 * lax.rem(me // 2**bit, 2)) * 2**bit for bit in range(global_bits)]
    peers = {
        step: me + sum(flips[bit] for bit in range(global_bits) if step >> bit & 1)
        for step in order
    }

    quarter = count // 4
    top, second_bit = lax.div(me, 2 * quarter), lax.rem(lax.div(me, quarter), 2)
    middle = top + second_bit - 2 * top * second_bit
    inner = middle == 1
    outer = middle == 0

    def greet(semaphore, step):
        pl.semaphore_signal(
            semaphore, inc=1, device_id={axis: peers[step]}, device_id_type=MESH
        )

    barrier = pltpu.get_barrier_semaphore()

    @pl.when(inner)
    def _():
        for step in range(3 * quarter, count):
            greet(barrier, step)

    for step in range(2 * quarter - 1, 0, -1):
        greet(barrier, step)
    arrivals = [
        pltpu.make_async_copy(source, target, local_sems.at[number])
        for number, (source, target) in enumerate(
            [
                (couple_hbm, couple_ref),
                (turn_hbm, turn_ref),
                (order_hbm, order_ref),
                (sign_hbm, sign_ref),
                (state_hbm, state_ref),
            ]
        )
    ]
    for copy in arrivals:
        copy.start()


    for entry in range(ANGLES):
        theta = (entry + 1) * math.pi / (2.0 * (ANGLES + 1))
        table[0, entry] = F32(math.cos(theta))
        table[1, entry] = F32(math.sin(theta))
    for copy in arrivals[:-1]:
        copy.wait()

    def turn(layer, qubit):
        index = turn_ref[layer, qubit]
        return table[0, index], table[1, index]

    height = -(-qubits // 8) * 8
    place = lax.broadcasted_iota(jnp.int32, (height, LANES), 0) * LANES + (
        lax.broadcasted_iota(jnp.int32, (height, LANES), 1)
    )

    def couplings(layers):
        matrices = [jnp.zeros((height, LANES), F32) for _ in layers]
        for bond in range(qubits - 1):
            start, end = order_ref[bond], order_ref[bond + 1]
            here = (place == start * LANES + end) | (place == end * LANES + start)
            for number, layer in enumerate(layers):
                value = (2 * sign_ref[bond] - 1).astype(F32)
                if layer < LAYERS:
                    value = angle(couple_ref[layer, bond]) * value
                matrices[number] = jnp.where(here, value, matrices[number])
        rest = jnp.zeros((LANES - height, LANES), F32)
        return [jnp.concatenate([matrix, rest], axis=0) for matrix in matrices]

    square_row = lax.broadcasted_iota(jnp.int32, (LANES, LANES), 0)
    square_lane = lax.broadcasted_iota(jnp.int32, (LANES, LANES), 1)
    lane_spin = (1 - 2 * ((square_lane >> jnp.minimum(square_row, 31)) & 1)).astype(F32)
    lane_only = jnp.where(square_row < LANE_BITS, lane_spin, 0.0)
    lane_ones = jnp.where(square_row < LANE_BITS, lane_spin, 1.0).astype(BF16)
    row_index = lax.broadcasted_iota(jnp.int32, (rows, LANES), 0)
    lane_index = lax.broadcasted_iota(jnp.int32, (rows, LANES), 1)

    def row_spin(swapped, chunked):
        held = row_index
        if chunked:
            inner = held & (chunk_rows - 1)
            block = (held >> inner_bits) & (count - 1)
            chunk = held >> (inner_bits + global_bits)
            held = inner + (chunk << inner_bits) + (block << low_bits)
        if swapped:
            low, high = held & (block_rows - 1), held >> low_bits
            index = low + (me << low_bits) + (high << row_bits)
        else:
            index = held + (me << row_bits)
        spin = (1 - 2 * ((index >> jnp.clip(lane_index - LANE_BITS, 0, 31)) & 1)).astype(F32)
        return jnp.where((lane_index >= LANE_BITS) & (lane_index < qubits), spin, 0.0)

    def field(spin, matrix, exact, half=None):
        if half is not None:
            pass
        elif exact:
            half = mm(spin.astype(BF16), matrix.astype(BF16))
        else:
            half = mm_exact_left(spin.astype(BF16), matrix)
        half = jnp.where(lane_index < LANE_BITS, half, 0.5 * half * spin)
        lane_pairs = 0.5 * jnp.sum(
            mm_exact_right(matrix[:TILE], lane_only.astype(BF16)) * lane_only[:TILE],
            axis=0,
            keepdims=True,
        )
        if exact:
            return mm(half.astype(BF16), lane_ones) + lane_pairs
        return mm_exact_right(half, lane_ones) + lane_pairs

    def copies(layer, unit, steps=None):
        return [
            pltpu.make_async_remote_copy(
                src_ref=send.at[layer, unit, peers[step]],
                dst_ref=recv.at[layer, unit, me],
                send_sem=send_sem,
                recv_sem=recv_sems.at[layer, unit],
                device_id={axis: peers[step]},
                device_id_type=MESH,
            )
            for step in (plans[layer][unit % 2] if steps is None else steps)
        ]

    def stat_copies(which):
        return [
            pltpu.make_async_remote_copy(
                src_ref=(norm_send, energy_send)[which],
                dst_ref=(norm_recv, energy_recv)[which].at[me],
                send_sem=stat_send_sems.at[which],
                recv_sem=stat_recv_sems.at[which],
                device_id={axis: peers[step]},
                device_id_type=MESH,
            )
            for step in order
        ]

    others = pl.ds(0, count - 1)

    def blocks(layer, unit):
        return pltpu.make_async_remote_copy(
            src_ref=send.at[layer, unit, others],
            dst_ref=recv.at[layer, unit, others],
            send_sem=send_sem,
            recv_sem=recv_sems.at[layer, unit],
            device_id={axis: peers[order[0]]},
            device_id_type=MESH,
        )

    def shelf(chunk):
        start = chunk % depth * TILE
        return slice(start, start + TILE)

    def received(layer, chunk):
        values = recv[layer, chunk // depth, :, shelf(chunk), :]
        return values.reshape(count * TILE, LANES)

    def stats(which):
        return pltpu.make_async_remote_copy(
            src_ref=(norm_recv, energy_recv)[which].at[others],
            dst_ref=(norm_recv, energy_recv)[which].at[others],
            send_sem=stat_send_sems.at[which],
            recv_sem=stat_recv_sems.at[which],
            device_id={axis: peers[order[0]]},
            device_id_type=MESH,
        )

    upper = lax.broadcasted_iota(jnp.int32, (TILE, LANES), 0) < TILE // 2
    side = jnp.where(upper, F32(1.0), F32(-1.0))

    def tile(values, number):
        return values[number * TILE : (number + 1) * TILE]

    def spread(values, signed):
        turned = flipped(values)
        found = []
        for number in range(tiles):
            here, there = tile(values, number // 2), tile(turned, number // 2)
            if number % 2:
                here, there = there, here
            both = jnp.where(upper, here, there)
            found.append(both * side if signed else both)
        return found

    def part(found, chunk):
        return jnp.concatenate(found[chunk * count : (chunk + 1) * count], axis=0)

    def ones(values, bits):
        return sum((values >> bit) & 1 for bit in range(bits))

    small_row = lax.broadcasted_iota(jnp.int32, (TILE, LANES), 0)
    small_lane = lax.broadcasted_iota(jnp.int32, (TILE, LANES), 1)
    held_ones = ones(small_lane, LANE_BITS) + sum(
        lax.rem(lax.div(me, 2**bit), 2) for bit in range(global_bits)
    )
    quarters = [
        ((held_ones + ones(small_row, 3) + more) & 3).astype(F32) * F32(-math.pi / 2)
        for more in range(4)
    ]
    frame = jnp.concatenate(
        [quarters[number.bit_count() & 3] for number in range(rows // TILE)], axis=0
    )

    def doubled(first, step):
        found = [first]
        for bit in range(3, row_bits):
            found = sum(zip(*[step(value, bit) for value in found]), ())
        return jnp.concatenate(found, axis=0)

    def own_spin(bit):
        if bit < row_bits:
            return (1 - 2 * ((small_row >> bit) & 1)).astype(F32)
        bit = bit - row_bits
        return (1 - 2 * lax.rem(lax.div(me, 2**bit), 2)).astype(F32)

    own_bits = list(range(3)) + list(range(row_bits, row_bits + global_bits))
    above = small_lane - LANE_BITS
    first_spin = jnp.where((above >= 0) & (above < row_bits), F32(1.0), F32(0.0))
    for bit in own_bits:
        first_spin = jnp.where(above == bit, own_spin(bit), first_spin)
    bonds = couplings([0])[0]

    def bond_row(bit):
        return bonds[LANE_BITS + bit : LANE_BITS + bit + 1]

    spin = doubled(
        first_spin,
        lambda value, bit: (value, jnp.where(above == bit, -value, value)),
    )
    half = doubled(
        sum(own_spin(bit) * bond_row(bit) for bit in own_bits),
        lambda value, bit: (value + bond_row(bit), value - bond_row(bit)),
    )
    sine, cosine = sin_cos(field(spin, bonds, False, half) + frame)
    lanes = right_operand(rotation([turn(0, qubit) for qubit in range(LANE_BITS)], True))
    held = split(rotation([turn(0, LANE_BITS + bit) for bit in range(row_bits)]))

    arrivals[-1].wait()
    real = state_ref[pl.ds(0, rows, 2), :]
    imag = state_ref[pl.ds(1, rows, 2), :]
    norm_send[...] = jnp.sum(real * real + imag * imag, axis=0, keepdims=True)
    real, imag = cosine * real + sine * imag, cosine * imag - sine * real
    both = apply_lanes(jnp.concatenate([real, imag], axis=0), lanes)
    both = mm3(held, split(jnp.concatenate([both[:rows], both[rows:]], axis=1)))
    real, imag = both[:, :LANES], both[:, LANES:]
    turned_real, turned_imag = flipped(real), flipped(imag)
    first = [copies(0, unit) if unit else [] for unit in range(units)]
    second = [copies(1, unit) for unit in range(units)]
    norms, weights = stat_copies(0), stat_copies(1)
    def pack(unit):
        for chunk in range(unit * depth, unit * depth + depth):
            for block in range(count):
                number = block * chunks + chunk
                if number % 2:
                    ends = tile(turned_real, number // 2), tile(imag, number // 2)
                else:
                    ends = tile(real, number // 2), tile(turned_imag, number // 2)
                send[0, unit, block, shelf(chunk), :] = jnp.where(upper, *ends)

    pack(0)
    def begin(groups):
        for group in groups:
            steps = [group * quarter + low for low in reversed(range(quarter))]
            for copy in copies(0, 0, [step for step in steps if step]):
                copy.start()

    pl.semaphore_wait(barrier, 2 * quarter - 1 + middle * quarter)

    @pl.when(inner)
    def _():
        greet(near_sem, 3 * quarter)
        greet(near_sem, quarter)
        begin((3,))

    begin((1, 0))
    for unit in range(1, units):
        pack(unit)
    pl.semaphore_wait(near_sem, 1)

    @pl.when(inner)
    def _():
        greet(far_sem, quarter)
        begin((2,))

    @pl.when(outer)
    def _():
        begin((2,))
        pl.semaphore_wait(far_sem, 1)
        begin((3,))

    for unit in range(units):
        recv[0, unit, me] = send[0, unit, me]
    norm_recv[me] = norm_send[...]

    moved = row_spin(True, True)
    next_bonds, sign_bonds = couplings([1, LAYERS])
    sine, cosine = sin_cos(field(moved, next_bonds, False))
    sine, cosine = spread(sine, True), spread(cosine, False)
    for unit in range(1, units):
        for copy in first[unit]:
            copy.start()
    for copy in norms:
        copy.start()
    lanes = right_operand(rotation([turn(1, qubit) for qubit in range(LANE_BITS)], True))
    held = jnp.concatenate(
        split(
            rotation(
                [turn(1, LANE_BITS + bit) for bit in range(inner_bits)]
                + [None]
                + [turn(1, local_bits + bit) for bit in range(global_bits)]
            )
        ),
        axis=1,
    )
    late = [turn(1, LANE_BITS + inner_bits + bit) for bit in range(chunk_bits)]
    tops = [
        [turn(0, local_bits + bit) for bit in range(global_bits)],
        [turn(1, local_bits - global_bits + bit) for bit in range(global_bits)],
    ]
    energy_moved = spread(field(moved, sign_bonds, True), False)
    energy_plain = spread(field(row_spin(False, True), sign_bonds, True), False)

    def folded(parts, energy_field):
        total = jnp.zeros((TILE, LANES), F32)
        for chunk, values in enumerate(parts):
            weight = values * values * part(energy_field, chunk)
            for block in range(count):
                total = total + tile(weight, block)
        return jnp.sum(total, axis=0, keepdims=True)

    between = []
    for chunk in range(chunks):
        if chunk % depth == 0:
            blocks(0, chunk // depth).wait_recv()
        values = turn_blocks(received(0, chunk), tops[0])
        between.append(values)
        values = part(cosine, chunk) * values + part(sine, chunk) * flipped(values)
        values = apply_lanes(values, lanes)
        values = paired(held, right_operand(values))
        unit = chunk // depth
        send[1, unit, :, shelf(chunk), :] = values.reshape(count, TILE, LANES)
        if chunk % depth == depth - 1:
            for copy in second[unit]:
                copy.start()
            recv[1, unit, me] = send[1, unit, me]

    energy_send[0:1] = folded(between, energy_moved)
    stats(0).wait_recv()
    amps_total = F32(2.0**qubits)
    norm = jnp.sum(jnp.sum(norm_recv[...], axis=0), axis=1, keepdims=True)
    factor = 1.0 / jnp.sqrt(norm / amps_total + 1e-06)
    phase = (held_ones + ones(small_row, inner_bits)) & 3
    even = (phase & 1) == 0
    sign = jnp.where((phase & 2) == 0, factor, -factor)
    along, across = jnp.where(even, sign, 0.0), jnp.where(even, 0.0, sign)
    frames = [
        (along, across * side),
        (-across, along * side),
        (-along, -across * side),
        (across, -along * side),
    ]

    parts = []
    for chunk in range(chunks):
        if chunk % depth == 0:
            blocks(1, chunk // depth).wait_recv()
        parts.append(turn_blocks(received(1, chunk), tops[1]))
        for bit, (cosine, sine) in enumerate(late):
            if (chunk + 1) % (2 << bit) == 0:
                for high in range(chunk + 1 - (1 << bit), chunk + 1):
                    low = high - (1 << bit)
                    parts[low], parts[high] = (
                        cosine * parts[low] - sine * parts[high],
                        cosine * parts[high] + sine * parts[low],
                    )

    energy_send[1:2] = folded(parts, energy_plain)
    for copy in weights:
        copy.start()
    energy_recv[me] = energy_send[...]
    for chunk, values in enumerate(parts):
        turned = flipped(values)
        for block in range(count):
            along, across = frames[(block.bit_count() + chunk.bit_count()) & 3]
            final = along * tile(values, block) + across * tile(turned, block)
            start = TILE * (block * chunks + chunk)
            out_ref[pl.ds(start, chunk_rows, 2), :] = final[:chunk_rows]
            out_ref[pl.ds(start + 1, chunk_rows, 2), :] = final[chunk_rows:]
    pltpu.make_async_remote_copy(
        src_ref=send.at[:, :, others],
        dst_ref=recv.at[:, :, others],
        send_sem=send_sem,
        recv_sem=recv_sems.at[0, 0],
        device_id={axis: peers[order[0]]},
        device_id_type=MESH,
    ).wait_send()
    stats(0).wait_send()
    stats(1).wait_recv()
    sums = jnp.sum(energy_recv[...], axis=0) * (factor * factor / amps_total)
    sums = jnp.sum(sums, axis=1, keepdims=True)
    which = lax.broadcasted_iota(jnp.int32, (1, LAYERS), 1)
    energy_ref[...] = jnp.where(which == 0, sums[0:1], sums[1:2])
    stats(1).wait_send()


def place(state_ref, energy_ref, state_out, energy_out, sems):
    moves = [
        pltpu.make_async_copy(state_ref, state_out, sems.at[0]),
        pltpu.make_async_copy(energy_ref, energy_out, sems.at[1]),
    ]
    for move in moves:
        move.start()
    for move in moves:
        move.wait()


def solution(mesh):
    axis = "amp"
    count = mesh.shape[axis]

    def local(amplitudes, coupling_index, rotation_index, chain_order, bond_sign):
        rows = amplitudes.shape[1] // LANES
        qubits = chain_order.shape[0]
        block_rows = rows // count
        chunk_rows = TILE // 2
        chunks = block_rows // chunk_rows
        depth = 2 if chunks % 2 == 0 else 1
        units = chunks // depth
        view = amplitudes.reshape(2, rows, LANES).transpose(1, 0, 2).reshape(2 * rows, LANES)
        vmem = pl.BlockSpec(memory_space=pltpu.VMEM)
        anywhere = pl.BlockSpec(memory_space=pl.ANY)
        state, energies = pl.pallas_call(
            functools.partial(kernel, axis, count, chunks, depth, qubits),
            out_shape=(
                pltpu.VMEM((2 * rows, LANES), F32),
                pltpu.VMEM((1, LAYERS), F32),
            ),
            in_specs=[anywhere] * 5,
            out_specs=(vmem, vmem),
            scratch_shapes=[
                pltpu.VMEM((2 * rows, LANES), F32),
                pltpu.SMEM(coupling_index.shape, jnp.int32),
                pltpu.SMEM(rotation_index.shape, jnp.int32),
                pltpu.SMEM(chain_order.shape, jnp.int32),
                pltpu.SMEM(bond_sign.shape, jnp.int32),
                pltpu.SMEM((2, ANGLES), F32),
                pltpu.VMEM((LAYERS, units, count, depth * TILE, LANES), F32),
                pltpu.VMEM((LAYERS, units, count, depth * TILE, LANES), F32),
                pltpu.VMEM((1, LANES), F32),
                pltpu.VMEM((count, 1, LANES), F32),
                pltpu.VMEM((LAYERS, LANES), F32),
                pltpu.VMEM((count, LAYERS, LANES), F32),
                pltpu.SemaphoreType.DMA((5,)),
                pltpu.SemaphoreType.DMA,
                pltpu.SemaphoreType.DMA((LAYERS, units)),
                pltpu.SemaphoreType.DMA((2,)),
                pltpu.SemaphoreType.DMA((2,)),
                pltpu.SemaphoreType.REGULAR,
                pltpu.SemaphoreType.REGULAR,
            ],
            compiler_params=pltpu.CompilerParams(collective_id=0, has_side_effects=True),
        )(view, coupling_index, rotation_index, chain_order, bond_sign)
        state, energies = pl.pallas_call(
            place,
            out_shape=(
                jax.ShapeDtypeStruct((2 * rows, LANES), F32),
                jax.ShapeDtypeStruct((1, LAYERS), F32),
            ),
            in_specs=[anywhere] * 2,
            out_specs=(anywhere, anywhere),
            scratch_shapes=[pltpu.SemaphoreType.DMA((2,))],
        )(*(pltpu.with_memory_space_constraint(x, pltpu.VMEM) for x in (state, energies)))
        state = state.reshape(rows, 2, LANES).transpose(1, 0, 2).reshape(2, rows * LANES)
        return state, energies.reshape(LAYERS)

    in_specs = (P(None, ("rep", "amp")), P("rep", None), P("rep", None), P(), P())
    out_specs = (P(None, ("rep", "amp")), P("rep"))
    return jax.shard_map(local, mesh=mesh, in_specs=in_specs, out_specs=out_specs, check_vma=False)
```

time: 24.9 us -> 24.6 us (0.988)
  Pallas kernels: 24.1 us -> 23.8 us
    pallas_call x1, Pallas kernels: 23.4 us -> 23.1 us  [local(): pl.pallas_call(functools.partial(kernel, axis, count, chunks, depth, qubi...]
where the time goes in v3:
time: 24.6 us; the launch traced here: 24.5 us
  Pallas kernels  23.8 us (97%)
  between operations  0.64 us (3%)
    pallas_call x1, Pallas kernels, local(): pl.pallas_call(functools.partial(kernel, axis, count, chunks, depth, qubi...  23.1 us
    pallas_call x1, Pallas kernels, local(): pl.pallas_call(place, out_shape=(jax.ShapeDtypeStruct((2 * rows, LANES),...  0.72 us

profile of v3, /device:TPU:0, one launch (start us, length us, event | category | flops | bytes accessed | tf_op | source)
XLA Modules:
  0.0 24.5 jit_solution(12696177686846371094)
XLA Ops:
  0.6 23.1 %shard_map.68 = (f32[512,128]{1,0:T(8,128)S(1)}, f32[1,2]{1,0:T(1,128)S(1)}) custom-call(f32[512,128]{1,0:T(8,128)} %bitcast.11, s32[2,18]{1,0:T(2,128)} %couple_hbm.1, s32[2,19]{1,0:T(2,128)} %turn_hbm.1, s32[19]{0:T(128)} %order_hbm.1, s32[18]{0:T(128)} %sign_hbm.1), custom_call_target="tpu_custom_call" | custom-call | tf_op jit(solution)/shard_map/pallas_call | solution.py:611
  23.7 0.7 %shard_map.69 = (f32[512,128]{1,0:T(8,128)}, f32[1,2]{1,0:T(1,128)}) custom-call(f32[512,128]{1,0:T(8,128)S(1)} %get-tuple-element.6.state_ref, f32[1,2]{1,0:T(1,128)S(1)} %get-tuple-element.7.energy_ref), custom_call_target="tpu_custom_call" | custom-call | tf_op jit(solution)/shard_map/pallas_call | solution.py:642

commit v4 on v3

--- a/solution.py
+++ b/solution.py
@@ -18,7 +18,11 @@
 MESH = pl.DeviceIdType.MESH
 DOWN = (3, 2, 1, 0)
 PLANS = (
-    (((2, 3, 1, 0), (2, 0, 3, 1)), ((1, 0, 2, 3), DOWN)),
+    (((2, 3, 1, 0), DOWN), ((1, 0, 2, 3), DOWN)),
+    (((2, 1, 3, 0), DOWN), ((2, 3, 0, 1), DOWN)),
+)
+INNER = (
+    (((2, 3, 1, 0), DOWN), ((1, 0, 2, 3), DOWN)),
     (((2, 3, 1, 0), DOWN), ((2, 3, 0, 1), DOWN)),
 )
 
@@ -176,7 +180,6 @@
         return [step for step in steps if step]
 
     order = ranked((2, 3, 1, 0), (3, 2, 1, 0))
-    plans = [[ranked(*plan) for plan in layer] for layer in PLANS]
     flips = [(1 - 2 * lax.rem(me // 2**bit, 2)) * 2**bit for bit in range(global_bits)]
     peers = {
         step: me + sum(flips[bit] for bit in range(global_bits) if step >> bit & 1)
@@ -288,7 +291,7 @@
             return mm(half.astype(BF16), lane_ones) + lane_pairs
         return mm_exact_right(half, lane_ones) + lane_pairs
 
-    def copies(layer, unit, steps=None):
+    def copies(layer, unit, steps):
         return [
             pltpu.make_async_remote_copy(
                 src_ref=send.at[layer, unit, peers[step]],
@@ -298,7 +301,7 @@
                 device_id={axis: peers[step]},
                 device_id_type=MESH,
             )
-            for step in (plans[layer][unit % 2] if steps is None else steps)
+            for step in steps
         ]
 
     def stat_copies(which):
@@ -423,8 +426,6 @@
     both = mm3(held, split(jnp.concatenate([both[:rows], both[rows:]], axis=1)))
     real, imag = both[:, :LANES], both[:, LANES:]
     turned_real, turned_imag = flipped(real), flipped(imag)
-    first = [copies(0, unit) if unit else [] for unit in range(units)]
-    second = [copies(1, unit) for unit in range(units)]
     norms, weights = stat_copies(0), stat_copies(1)
     def pack(unit):
         for chunk in range(unit * depth, unit * depth + depth):
@@ -437,6 +438,13 @@
                 send[0, unit, block, shelf(chunk), :] = jnp.where(upper, *ends)
 
     pack(0)
+    def launch(layer, unit):
+        for place, plan in ((outer, PLANS[layer][unit % 2]), (inner, INNER[layer][unit % 2])):
+            @pl.when(place)
+            def _():
+                for copy in copies(layer, unit, ranked(*plan)):
+                    copy.start()
+
     def begin(groups):
         for group in groups:
             steps = [group * quarter + low for low in reversed(range(quarter))]
@@ -476,8 +484,7 @@
     sine, cosine = sin_cos(field(moved, next_bonds, False))
     sine, cosine = spread(sine, True), spread(cosine, False)
     for unit in range(1, units):
-        for copy in first[unit]:
-            copy.start()
+        launch(0, unit)
     for copy in norms:
         copy.start()
     lanes = right_operand(rotation([turn(1, qubit) for qubit in range(LANE_BITS)], True))
@@ -519,8 +526,7 @@
         unit = chunk // depth
         send[1, unit, :, shelf(chunk), :] = values.reshape(count, TILE, LANES)
         if chunk % depth == depth - 1:
-            for copy in second[unit]:
-                copy.start()
+            launch(1, unit)
             recv[1, unit, me] = send[1, unit, me]
 
     energy_send[0:1] = folded(between, energy_moved)

time: 24.6 us -> 24.4 us (level)
  no operation moved by 1% of the time
where the time goes in v4:
time: 24.4 us; the launch traced here: 24.3 us
  Pallas kernels  23.7 us (97%)
  between operations  0.64 us (3%)
    pallas_call x1, Pallas kernels, local(): pl.pallas_call(functools.partial(kernel, axis, count, chunks, depth, qubi...  22.9 us
    pallas_call x1, Pallas kernels, local(): pl.pallas_call(place, out_shape=(jax.ShapeDtypeStruct((2 * rows, LANES),...  0.72 us

profile of v4, /device:TPU:0, one launch (start us, length us, event | category | flops | bytes accessed | tf_op | source)
XLA Modules:
  0.0 24.3 jit_solution(10520932118202650377)
XLA Ops:
  0.6 22.9 %shard_map.68 = (f32[512,128]{1,0:T(8,128)S(1)}, f32[1,2]{1,0:T(1,128)S(1)}) custom-call(f32[512,128]{1,0:T(8,128)} %bitcast.11, s32[2,18]{1,0:T(2,128)} %couple_hbm.1, s32[2,19]{1,0:T(2,128)} %turn_hbm.1, s32[19]{0:T(128)} %order_hbm.1, s32[18]{0:T(128)} %sign_hbm.1), custom_call_target="tpu_custom_call" | custom-call | tf_op jit(solution)/shard_map/pallas_call | solution.py:617
  23.6 0.7 %shard_map.69 = (f32[512,128]{1,0:T(8,128)}, f32[1,2]{1,0:T(1,128)}) custom-call(f32[512,128]{1,0:T(8,128)S(1)} %get-tuple-element.6.state_ref, f32[1,2]{1,0:T(1,128)S(1)} %get-tuple-element.7.energy_ref), custom_call_target="tpu_custom_call" | custom-call | tf_op jit(solution)/shard_map/pallas_call | solution.py:648

commit v5 on v4

--- a/solution.py
+++ b/solution.py
@@ -57,7 +57,8 @@
     rest = values - high.astype(F32)
     middle = rest.astype(BF16)
     low = (rest - middle.astype(F32)).astype(BF16)
-    return mm(high, right) + mm(middle, right) + mm(low, right)
+    joined = jnp.concatenate([high, middle], axis=1)
+    return mm(joined, jnp.concatenate([right, right], axis=0)) + mm(low, right)
 
 
 def sin_cos(values):

time: 24.4 us -> 24.6 us (level)
  no operation moved by 1% of the time
where the time goes in v5:
time: 24.6 us; the launch traced here: 24.4 us
  Pallas kernels  23.8 us (97%)
  between operations  0.64 us (3%)
    pallas_call x1, Pallas kernels, local(): pl.pallas_call(functools.partial(kernel, axis, count, chunks, depth, qubi...  23.1 us
    pallas_call x1, Pallas kernels, local(): pl.pallas_call(place, out_shape=(jax.ShapeDtypeStruct((2 * rows, LANES),...  0.72 us

profile of v5, /device:TPU:0, one launch (start us, length us, event | category | flops | bytes accessed | tf_op | source)
XLA Modules:
  0.0 24.4 jit_solution(5743975742238025569)
XLA Ops:
  0.6 23.1 %shard_map.68 = (f32[512,128]{1,0:T(8,128)S(1)}, f32[1,2]{1,0:T(1,128)S(1)}) custom-call(f32[512,128]{1,0:T(8,128)} %bitcast.11, s32[2,18]{1,0:T(2,128)} %couple_hbm.1, s32[2,19]{1,0:T(2,128)} %turn_hbm.1, s32[19]{0:T(128)} %order_hbm.1, s32[18]{0:T(128)} %sign_hbm.1), custom_call_target="tpu_custom_call" | custom-call | tf_op jit(solution)/shard_map/pallas_call | solution.py:618
  23.7 0.7 %shard_map.69 = (f32[512,128]{1,0:T(8,128)}, f32[1,2]{1,0:T(1,128)}) custom-call(f32[512,128]{1,0:T(8,128)S(1)} %get-tuple-element.6.state_ref, f32[1,2]{1,0:T(1,128)S(1)} %get-tuple-element.7.energy_ref), custom_call_target="tpu_custom_call" | custom-call | tf_op jit(solution)/shard_map/pallas_call | solution.py:649

commit v6 on v4

--- a/solution.py
+++ b/solution.py
@@ -199,13 +199,6 @@
 
     barrier = pltpu.get_barrier_semaphore()
 
-    @pl.when(inner)
-    def _():
-        for step in range(3 * quarter, count):
-            greet(barrier, step)
-
-    for step in range(2 * quarter - 1, 0, -1):
-        greet(barrier, step)
     arrivals = [
         pltpu.make_async_copy(source, target, local_sems.at[number])
         for number, (source, target) in enumerate(
@@ -220,6 +213,14 @@
     ]
     for copy in arrivals:
         copy.start()
+
+    @pl.when(inner)
+    def _():
+        for step in range(3 * quarter, count):
+            greet(barrier, step)
+
+    for step in range(2 * quarter - 1, 0, -1):
+        greet(barrier, step)
 
 
     for entry in range(ANGLES):

time: 24.4 us -> 24.4 us (level)
  no operation moved by 1% of the time
where the time goes in v6:
time: 24.4 us; the launch traced here: 24.3 us
  Pallas kernels  23.7 us (97%)
  between operations  0.64 us (3%)
    pallas_call x1, Pallas kernels, local(): pl.pallas_call(functools.partial(kernel, axis, count, chunks, depth, qubi...  22.9 us
    pallas_call x1, Pallas kernels, local(): pl.pallas_call(place, out_shape=(jax.ShapeDtypeStruct((2 * rows, LANES),...  0.72 us

profile of v6, /device:TPU:0, one launch (start us, length us, event | category | flops | bytes accessed | tf_op | source)
XLA Modules:
  0.0 24.3 jit_solution(12657751674814803917)
XLA Ops:
  0.6 22.9 %shard_map.68 = (f32[512,128]{1,0:T(8,128)S(1)}, f32[1,2]{1,0:T(1,128)S(1)}) custom-call(f32[512,128]{1,0:T(8,128)} %bitcast.11, s32[2,18]{1,0:T(2,128)} %couple_hbm.1, s32[2,19]{1,0:T(2,128)} %turn_hbm.1, s32[19]{0:T(128)} %order_hbm.1, s32[18]{0:T(128)} %sign_hbm.1), custom_call_target="tpu_custom_call" | custom-call | tf_op jit(solution)/shard_map/pallas_call | solution.py:618
  23.6 0.7 %shard_map.69 = (f32[512,128]{1,0:T(8,128)}, f32[1,2]{1,0:T(1,128)}) custom-call(f32[512,128]{1,0:T(8,128)S(1)} %get-tuple-element.6.state_ref, f32[1,2]{1,0:T(1,128)S(1)} %get-tuple-element.7.energy_ref), custom_call_target="tpu_custom_call" | custom-call | tf_op jit(solution)/shard_map/pallas_call | solution.py:649
